TPU v7x, 32 devices: a whole 2x2x4 slice. The times are simulated.
32 devices in a mesh: wide: 4 (over x, core), narrow: 8 (over z, y).
Axes of the slice: x: 2, y: 2, z: 4, core: 2. Of those that a mesh axis runs over, the one named last changes fastest.
Arguments:
- velocity: float32 [3, 1, 4096, 4096], P(None, None, ('wide', 'narrow')), may hold values from -6 to 6
- plane_wavenumber: float32 [1], replicated, may hold values from 2 to 1024
Outputs:
- projected: float32 [3, 1, 4096, 4096], P(None, None, ('wide', 'narrow'))
All inputs are finite; a program needn't handle non-finite values.
Results may differ from a plain program's by a relative error of at most 0.00007.
Values sent between devices are 32-bit elements; how exact they have to be, the bound alone decides.
No kernel may reach another device: no remote copies, remote signals or barrier semaphores. Data moves between devices by JAX's collectives and lax.ppermute only.
A program may use at most 128 MiB of HBM per device.

v0:
```python
import math
import jax
import jax.numpy as jnp
from jax import lax
from jax.sharding import PartitionSpec as P

radix_split = 64
highest = lax.Precision.HIGHEST


def angle_tables(row_size, col_size, period, direction):
    product = jnp.arange(row_size)[:, None] * jnp.arange(col_size)[None, :] % period
    angles = direction * 2.0 * math.pi * product.astype(jnp.float32) / period
    return (jnp.cos(angles), jnp.sin(angles))


def complex_product(pattern, left_real, left_imag, table_real, table_imag):
    out_real = jnp.einsum(pattern, left_real, table_real, precision=highest) - jnp.einsum(
        pattern, left_imag, table_imag, precision=highest
    )
    out_imag = jnp.einsum(pattern, left_real, table_imag, precision=highest) + jnp.einsum(
        pattern, left_imag, table_real, precision=highest
    )
    return (out_real, out_imag)


def transform(real_part, imag_part, direction):
    length = real_part.shape[-1]
    inner_size = length // radix_split
    leading = real_part.shape[:-1]
    grid_real = real_part.reshape(leading + (radix_split, inner_size))
    grid_imag = imag_part.reshape(leading + (radix_split, inner_size))
    outer_cos, outer_sin = angle_tables(radix_split, radix_split, radix_split, direction)
    section_real, section_imag = complex_product(
        "...ab,ak->...kb", grid_real, grid_imag, outer_cos, outer_sin
    )
    twist_cos, twist_sin = angle_tables(radix_split, inner_size, length, direction)
    turned_real = section_real * twist_cos - section_imag * twist_sin
    turned_imag = section_real * twist_sin + section_imag * twist_cos
    inner_cos, inner_sin = angle_tables(inner_size, inner_size, inner_size, direction)
    final_real, final_imag = complex_product(
        "...kb,bm->...mk", turned_real, turned_imag, inner_cos, inner_sin
    )
    return (final_real.reshape(leading + (length,)), final_imag.reshape(leading + (length,)))


def project(lines, wave_x, wave_z, kept_line):
    groups, per_device, length_y = lines.shape
    shaped = lines.reshape(3, 2, groups // 6, per_device, length_y)
    spec_real, spec_imag = transform(shaped[:, 0], shaped[:, 1], -1.0)
    index_y = jnp.arange(length_y)
    signed_y = jnp.where(index_y <= length_y // 2, index_y, index_y - length_y)
    kept_y = jnp.abs(signed_y) <= length_y // 3
    retained = (kept_line & kept_y[None, None, :]).astype(jnp.float32)
    wave_y = signed_y.astype(jnp.float32)[None, None, :]
    wave_square = wave_x * wave_x + wave_y * wave_y + wave_z * wave_z
    waves = (wave_x, wave_y, wave_z)
    div_real = wave_x * spec_real[0] + wave_y * spec_real[1] + wave_z * spec_real[2]
    div_imag = wave_x * spec_imag[0] + wave_y * spec_imag[1] + wave_z * spec_imag[2]
    proj_real = jnp.stack(
        [
            (spec_real[component] - waves[component] * div_real / wave_square) * retained
            for component in range(3)
        ]
    )
    proj_imag = jnp.stack(
        [
            (spec_imag[component] - waves[component] * div_imag / wave_square) * retained
            for component in range(3)
        ]
    )
    back_real, back_imag = transform(proj_real, proj_imag, 1.0)
    return jnp.stack([back_real / length_y, back_imag / length_y], axis=1).reshape(
        groups, per_device, length_y
    )


def first_send(spectrum, first_size):
    groups, rows, span = spectrum.shape
    return (
        spectrum.reshape(groups, rows, first_size, span // first_size)
        .transpose(2, 0, 1, 3)
        .reshape(first_size, 1, -1)
    )


def second_send(received, first_size, second_size, groups, rows, per_device):
    shaped = received.reshape(first_size, groups, rows, second_size, per_device)
    return shaped.transpose(3, 1, 4, 0, 2).reshape(second_size, 1, -1)


def arrange_lines(received, first_size, second_size, groups, rows, per_device):
    shaped = received.reshape(second_size, groups, per_device, first_size, rows)
    ordered = shaped.transpose(1, 2, 0, 3, 4)
    return ordered.reshape(groups, per_device, -1)


def first_return(solved, first_size, second_size, rows):
    groups, per_device, _ = solved.shape
    shaped = solved.reshape(groups, per_device, second_size, first_size, rows).transpose(
        2, 0, 1, 3, 4
    )
    return shaped.reshape(second_size, 1, -1)


def second_return(received, first_size, second_size, groups, rows, per_device):
    shaped = received.reshape(second_size, groups, per_device, first_size, rows)
    return shaped.transpose(3, 1, 4, 0, 2).reshape(first_size, 1, -1)


def arrange_rows(received, first_size, groups, rows):
    shaped = received.reshape(first_size, groups, rows, -1)
    return shaped.transpose(1, 2, 0, 3).reshape(groups, rows, -1)


def local(velocity, plane_wavenumber):
    components, plane_count, row_count, x_length = velocity.shape
    wide_size = lax.axis_size("wide")
    narrow_size = lax.axis_size("narrow")
    device_count = wide_size * narrow_size
    keep_x = x_length // 3 + 1
    spec_real, spec_imag = transform(velocity, jnp.zeros_like(velocity), -1.0)
    spec_real = spec_real[..., :keep_x]
    spec_imag = spec_imag[..., :keep_x]
    per_device = (keep_x + device_count - 1) // device_count
    line_span = per_device * device_count
    gap = ((0, 0), (0, 0), (0, 0), (0, 0), (0, line_span - keep_x))
    stacked = jnp.stack([spec_real, spec_imag], axis=1)
    spectrum = jnp.pad(stacked, gap).reshape(components * 2 * plane_count, row_count, line_span)
    groups = spectrum.shape[0]
    halfway = lax.all_to_all(
        first_send(spectrum, narrow_size), "narrow", split_axis=0, concat_axis=1, tiled=True
    )
    outgoing = second_send(halfway, narrow_size, wide_size, groups, row_count, per_device)
    arrived = lax.all_to_all(outgoing, "wide", split_axis=0, concat_axis=1, tiled=True)
    lines = arrange_lines(arrived, narrow_size, wide_size, groups, row_count, per_device)
    line_start = (
        lax.axis_index("narrow") * (per_device * wide_size) + lax.axis_index("wide") * per_device
    )
    indices = line_start + jnp.arange(per_device)
    wave_x = indices.astype(jnp.float32)[None, :, None]
    wave_z = plane_wavenumber[:, None, None]
    kept_line = (indices < keep_x)[None, :, None]
    solved = project(lines, wave_x, wave_z, kept_line)
    halfway = lax.all_to_all(
        first_return(solved, narrow_size, wide_size, row_count),
        "wide",
        split_axis=0,
        concat_axis=1,
        tiled=True,
    )
    outgoing = second_return(halfway, narrow_size, wide_size, groups, row_count, per_device)
    arrived = lax.all_to_all(outgoing, "narrow", split_axis=0, concat_axis=1, tiled=True)
    returned = arrange_rows(arrived, narrow_size, groups, row_count)
    columns = returned.reshape(components, 2, plane_count, row_count, line_span)[..., :keep_x]
    weights = jnp.where(jnp.arange(keep_x) == 0, 1.0, 2.0).astype(jnp.float32)
    widen = ((0, 0), (0, 0), (0, 0), (0, x_length - keep_x))
    back_real = jnp.pad(columns[:, 0] * weights, widen)
    back_imag = jnp.pad(columns[:, 1] * weights, widen)
    out_real, out_imag = transform(back_real, back_imag, 1.0)
    return out_real / x_length


def solution(mesh):
    placed = (P(None, None, ("wide", "narrow"), None), P())
    return jax.shard_map(
        local,
        mesh=mesh,
        in_specs=placed,
        out_specs=P(None, None, ("wide", "narrow"), None),
        check_vma=False,
    )
```

profile of v0, /device:TPU:0, one launch (start us, length us, event | category | flops | bytes accessed | tf_op | source)
XLA Modules:
  0.0 851.3 jit_solution(1181814289955283655)
XLA Ops:
  9.5 6.6 copy.55
  16.1 13.6 %fusion.28 = f32[64,3,128,64]{2,0,3,1:T(8,128)} fusion(f32[3,128,64,64]{1,3,2,0:T(8,128)} %bitcast.346), kind=kOutput, calls=%fused_computation.39 | convolution fusion | flops 1208016896 | bytes 12582912 | tf_op jit(solution)/shard_map/...ab,ak->...kb/dot_general | solution.py:21
  29.7 19.1 %fusion.5 = (f32[3,128,64,64]{1,2,3,0:T(8,128)}, f32[3,128,64,64]{1,2,3,0:T(8,128)S(1)}) fusion(f32[64,64]{0,1:T(8,128)S(1)} %get-tuple-element.25, f32[64,64]{0,1:T(8,128)S(1)} %get-tuple-element.26, f32[64,3,128,64]{2,0,3,1:T(8,128)} %fusion.28, f32[64,3,128,64]{2,0,3,1:T(8,128)} %fusion.52, f32[64,3,128,64]{2,0,3,1:T(8,128)} %fusion.54, ...), kind=kOutput, calls=%fused_computation.11 | convolution fusion | flops 1220599808 | bytes 37781504 | tf_op jit(solution)/shard_map/...ab,ak->...kb/dot_general | solution.py:18
  48.8 9.5 %fusion.22 = f32[64,3,128,64]{2,0,3,1:T(8,128)S(1)} fusion(f32[3,128,64,64]{1,2,3,0:T(8,128)S(1)} %get-tuple-element.12), kind=kOutput, calls=%fused_computation.33 | convolution fusion | flops 1208016896 | bytes 12582912 | tf_op jit(solution)/shard_map/...kb,bm->...mk/dot_general | solution.py:18
  58.3 9.6 %fusion.20 = f32[64,3,128,64]{2,0,3,1:T(8,128)S(1)} fusion(f32[3,128,64,64]{1,2,3,0:T(8,128)S(1)} %get-tuple-element.12), kind=kOutput, calls=%fused_computation.31 | convolution fusion | flops 1208016896 | bytes 12582912 | tf_op jit(solution)/shard_map/...kb,bm->...mk/dot_general | solution.py:21
  68.0 9.7 %subtract_bitcast_fusion = f32[3,1,128,64,64]{2,3,4,0,1:T(8,128)S(1)} fusion(f32[64,3,128,64]{2,0,3,1:T(8,128)S(1)} %fusion.22, f32[3,128,64,64]{1,2,3,0:T(8,128)S(1)} %bitcast.349), kind=kOutput, calls=%fused_computation.22 | convolution fusion | flops 1209589760 | bytes 18874368 | tf_op jit(solution)/shard_map/...kb,bm->...mk/dot_general | solution.py:18
  81.5 10.0 %add_bitcast_fusion = f32[3,1,128,64,64]{2,3,4,0,1:T(8,128)S(1)} fusion(f32[64,3,128,64]{2,0,3,1:T(8,128)S(1)} %fusion.20, f32[3,128,64,64]{1,2,3,0:T(8,128)S(1)} %bitcast.349), kind=kOutput, calls=%fused_computation.21 | convolution fusion | flops 1209589760 | bytes 18874368 | tf_op jit(solution)/shard_map/...kb,bm->...mk/dot_general | solution.py:21
  102.9 6.1 copy.65
  109.1 12.0 %reshape.976 = f32[8,1,132096]{2,1,0:T(1,128)} reshape(f32[8,6,128,172]{3,2,1,0:T(8,128)} %copy.65) | data formatting | bytes 8454144 | tf_op jit(solution)/shard_map/reshape | solution.py:83
  121.0 102.0 %all_to_all.16 = f32[8,1,132096]{2,1,0:T(1,128)} all-to-all(f32[8,1,132096]{2,1,0:T(1,128)} %reshape.976), channel_id=1, replica_groups=mesh['wide'=4,'narrow'=8] {'narrow'}, dimensions={0} | all-to-all | bytes 8454144 | tf_op jit(solution)/shard_map/all_to_all | solution.py:131
  223.0 13.4 %reduce = f32[8,132096]{1,0:T(8,128)} reduce(f32[8,1,132096]{2,1,0:T(1,128)} %all_to_all.16, f32[]{:T(128)} %constant.129), dimensions={1}, to_apply=%all_to_all.8.reduce_sub_computation | reduce | bytes 8454148 | tf_op jit(solution)/shard_map/all_to_all | solution.py:131
  236.4 26.8 %reshape.953 = f32[8,6,128,4,43]{4,3,2,1,0:T(4,128)} reshape(f32[8,132096]{1,0:T(8,128)} %reduce) | data formatting | bytes 8454144 | tf_op jit(solution)/shard_map/reshape | solution.py:88
  263.2 9.2 %copy.67 = f32[4,6,43,8,128]{4,3,2,1,0:T(8,128)} copy(f32[4,6,43,8,128]{2,0,4,1,3:T(4,128)} %bitcast.354) | data formatting | bytes 8454144 | tf_op jit(solution)/shard_map/transpose | solution.py:89
  272.5 5.1 all-to-all-start.1
  279.0 47.0 %all-to-all-done.1 = f32[4,1,264192]{2,1,0:T(1,128)} async-done(((f32[4,1,264192]{2,1,0:T(1,128)}), f32[4,1,264192]{2,1,0:T(1,128)}, u32[]{:S(2)}, u32[]{:S(2)}) %all-to-all-start.1) | async-done | bytes 4227104 | tf_op jit(solution)/shard_map/all_to_all | solution.py:135
  326.1 4.8 copy.134
  330.9 5.8 reshape_reshape.13
  336.7 9.3 %fusion.259 = (f32[3,1,1,43,4096]{4,1,0,3,2:T(1,128)}, f32[3,1,1,43,4096]{4,1,0,3,2:T(1,128)S(1)}) fusion(f32[3,2,1,43,4096]{4,1,0,3,2:T(2,128)} %reshape_reshape.13), kind=kLoop, calls=%fused_computation.298 | loop fusion | bytes 8454144 | tf_op jit(solution)/shard_map/slice | solution.py:50
  351.5 8.2 fusion.107
  359.7 6.0 fusion.97
  371.0 7.9 convolution_subtract_fusion
  383.4 11.3 %fusion.42 = f32[64,3,43,64]{3,0,2,1:T(8,128)S(1)} fusion(f32[64,3,43,64]{3,0,2,1:T(8,128)S(1)} %convolution_add_fusion, f32[64,3,43,64]{3,0,2,1:T(8,128)S(1)} %convolution_subtract_fusion, f32[64,64]{1,0:T(8,128)S(1)} %copy.73, f32[64,64]{1,0:T(8,128)S(1)} %copy.72), kind=kOutput, calls=%fused_computation.60 | convolution fusion | flops 407441408 | bytes 6373376 | tf_op jit(solution)/shard_map/...kb,bm->...mk/dot_general | solution.py:21
  394.8 11.5 %fusion.44 = f32[64,3,43,64]{3,0,2,1:T(8,128)S(1)} fusion(f32[64,3,43,64]{3,0,2,1:T(8,128)S(1)} %convolution_add_fusion, f32[64,3,43,64]{3,0,2,1:T(8,128)S(1)} %convolution_subtract_fusion, f32[64,64]{1,0:T(8,128)S(1)} %copy.73, f32[64,64]{1,0:T(8,128)S(1)} %copy.72), kind=kOutput, calls=%fused_computation.62 | convolution fusion | flops 407441408 | bytes 6373376 | tf_op jit(solution)/shard_map/...kb,bm->...mk/dot_general | solution.py:18
  406.3 11.1 %add_bitcast_fusion.1 = f32[3,1,43,64,64]{4,3,2,0,1:T(8,128)S(1)} fusion(f32[64,3,43,64]{3,0,2,1:T(8,128)S(1)} %fusion.42, f32[64,3,43,64]{3,0,2,1:T(8,128)S(1)} %convolution_add_fusion, f32[64,3,43,64]{3,0,2,1:T(8,128)S(1)} %convolution_subtract_fusion, f32[64,64]{1,0:T(8,128)S(1)} %copy.73, f32[64,64]{1,0:T(8,128)S(1)} %copy.72), kind=kOutput, calls=%fused_computation.77 | convolution fusion | flops 407969792 | bytes 8486912 | tf_op jit(solution)/shard_map/...kb,bm->...mk/dot_general | solution.py:21
  417.4 11.3 %subtract_bitcast_fusion.1 = f32[3,1,43,64,64]{4,3,2,0,1:T(8,128)S(1)} fusion(f32[64,3,43,64]{3,0,2,1:T(8,128)S(1)} %fusion.44, f32[64,3,43,64]{3,0,2,1:T(8,128)S(1)} %convolution_add_fusion, f32[64,3,43,64]{3,0,2,1:T(8,128)S(1)} %convolution_subtract_fusion, f32[64,64]{1,0:T(8,128)S(1)} %copy.73, f32[64,64]{1,0:T(8,128)S(1)} %copy.72), kind=kOutput, calls=%fused_computation.78 | convolution fusion | flops 407969792 | bytes 8486912 | tf_op jit(solution)/shard_map/...kb,bm->...mk/dot_general | solution.py:18
  449.6 11.3 %fusion.34 = f32[64,3,43,64]{3,0,2,1:T(8,128)S(1)} fusion(f32[64,3,43,64]{3,0,2,1:T(8,128)S(1)} %fusion.67, f32[64,3,43,64]{3,0,2,1:T(8,128)S(1)} %fusion.66, f32[64,64]{1,0:T(8,128)S(1)} %copy.77, f32[64,64]{1,0:T(8,128)S(1)} %copy.76), kind=kOutput, calls=%fused_computation.48 | convolution fusion | flops 407441408 | bytes 6373376 | tf_op jit(solution)/shard_map/...kb,bm->...mk/dot_general | solution.py:18
  460.9 13.1 %fusion.32 = f32[64,3,43,64]{3,0,2,1:T(8,128)} fusion(f32[64,3,43,64]{3,0,2,1:T(8,128)S(1)} %fusion.67, f32[64,3,43,64]{3,0,2,1:T(8,128)S(1)} %fusion.66, f32[64,64]{1,0:T(8,128)S(1)} %copy.77, f32[64,64]{1,0:T(8,128)S(1)} %copy.76), kind=kOutput, calls=%fused_computation.46 | convolution fusion | flops 407441408 | bytes 6373376 | tf_op jit(solution)/shard_map/...kb,bm->...mk/dot_general | solution.py:21
  473.9 13.3 %multiply_bitcast_fusion.2 = f32[3,1,43,64,64]{4,3,2,0,1:T(8,128)} fusion(f32[64,3,43,64]{3,0,2,1:T(8,128)S(1)} %fusion.34, f32[64,3,43,64]{3,0,2,1:T(8,128)S(1)} %fusion.67, f32[64,3,43,64]{3,0,2,1:T(8,128)S(1)} %fusion.66, f32[64,64]{1,0:T(8,128)S(1)} %copy.77, f32[64,64]{1,0:T(8,128)S(1)} %copy.76), kind=kOutput, calls=%fused_computation.76 | convolution fusion | flops 408498176 | bytes 8486912 | tf_op jit(solution)/shard_map/...kb,bm->...mk/dot_general | solution.py:18
  487.3 5.0 div.201
  492.3 17.7 %multiply_bitcast_fusion.1 = f32[3,1,43,64,64]{4,3,2,0,1:T(8,128)} fusion(f32[64,3,43,64]{3,0,2,1:T(8,128)} %fusion.32, f32[64,3,43,64]{3,0,2,1:T(8,128)} %copy-done.1, f32[64,3,43,64]{3,0,2,1:T(8,128)} %copy-done, f32[64,64]{1,0:T(8,128)S(1)} %copy.77, f32[64,64]{1,0:T(8,128)S(1)} %copy.76), kind=kOutput, calls=%fused_computation.75 | convolution fusion | flops 408498176 | bytes 8486912 | tf_op jit(solution)/shard_map/...kb,bm->...mk/dot_general | solution.py:21
  510.0 5.7 div.205
  515.7 5.9 pad_maximum_fusion
  525.2 6.7 reshape_reshape.14
  534.3 52.0 %all_to_all.17 = f32[4,1,264192]{2,1,0:T(1,128)} all-to-all(f32[4,1,264192]{2,1,0:T(1,128)S(1)} %bitcast.365), channel_id=1, replica_groups=mesh['wide'=4,'narrow'=8] {'wide'}, dimensions={0} | all-to-all | bytes 8454144 | tf_op jit(solution)/shard_map/all_to_all | solution.py:145
  586.3 9.0 %copy.81 = f32[4,6,43,8,128]{2,0,4,1,3:T(4,128)} copy(f32[4,6,43,8,128]{4,3,2,1,0:T(8,128)} %bitcast.367) | data formatting | bytes 8454144 | tf_op jit(solution)/shard_map/reshape | solution.py:107
  595.3 20.3 %reshape.977 = f32[8,1,132096]{2,1,0:T(1,128)} reshape(f32[8,6,128,4,43]{4,3,2,1,0:T(4,128)} %bitcast.355) | data formatting | bytes 8454144 | tf_op jit(solution)/shard_map/reshape | solution.py:108
  620.4 94.2 %all-to-all-done.3 = f32[8,1,132096]{2,1,0:T(1,128)} async-done(((f32[8,1,132096]{2,1,0:T(1,128)}), f32[8,1,132096]{2,1,0:T(1,128)}, u32[]{:S(2)}, u32[]{:S(2)}) %all-to-all-start.3) | async-done | bytes 4227104 | tf_op jit(solution)/shard_map/all_to_all | solution.py:153
  714.6 13.2 %reduce.1 = f32[8,132096]{1,0:T(8,128)} reduce(f32[8,1,132096]{2,1,0:T(1,128)} %all-to-all-done.3, f32[]{:T(128)} %constant.129), dimensions={1}, to_apply=%all_to_all.11.reduce_sub_computation | reduce | bytes 8454148 | tf_op jit(solution)/shard_map/all_to_all | solution.py:153
  727.8 13.7 %reshape.967 = f32[8,6,128,172]{3,2,1,0:T(8,128)} reshape(f32[8,132096]{1,0:T(8,128)} %reduce.1) | data formatting | bytes 8454144 | tf_op jit(solution)/shard_map/reshape | solution.py:112
  741.5 6.0 copy.83
  755.3 13.5 %fusion.12 = f32[64,3,128,64]{2,0,3,1:T(8,128)} fusion(f32[3,128,64,64]{1,3,2,0:T(8,128)S(1)} %bitcast.352), kind=kOutput, calls=%fused_computation.23 | convolution fusion | flops 1208016896 | bytes 12582912 | tf_op jit(solution)/shard_map/...ab,ak->...kb/dot_general | solution.py:21
  768.8 13.0 %fusion.14 = f32[64,3,128,64]{2,0,3,1:T(8,128)} fusion(f32[3,128,64,64]{1,3,2,0:T(8,128)S(1)} %bitcast.353), kind=kOutput, calls=%fused_computation.25 | convolution fusion | flops 1208016896 | bytes 12582912 | tf_op jit(solution)/shard_map/...ab,ak->...kb/dot_general | solution.py:18
  782.1 13.2 %fusion.16 = f32[64,3,128,64]{2,0,3,1:T(8,128)} fusion(f32[3,128,64,64]{1,3,2,0:T(8,128)S(1)} %bitcast.350), kind=kOutput, calls=%fused_computation.27 | convolution fusion | flops 1208016896 | bytes 12582912 | tf_op jit(solution)/shard_map/...ab,ak->...kb/dot_general | solution.py:21
  795.3 19.8 %fusion.1 = (f32[3,128,64,64]{1,2,3,0:T(8,128)}, f32[3,128,64,64]{1,2,3,0:T(8,128)}) fusion(f32[64,64]{0,1:T(8,128)S(1)} %get-tuple-element.27, f32[64,64]{0,1:T(8,128)S(1)} %get-tuple-element.28, f32[64,3,128,64]{2,0,3,1:T(8,128)} %fusion.16, f32[64,3,128,64]{2,0,3,1:T(8,128)} %fusion.12, f32[64,3,128,64]{2,0,3,1:T(8,128)} %fusion.14, ...), kind=kOutput, calls=%fused_computation.3 | convolution fusion | flops 1220599808 | bytes 37781504 | tf_op jit(solution)/shard_map/...ab,ak->...kb/dot_general | solution.py:18
  815.2 12.6 %fusion.8 = f32[64,3,128,64]{2,0,3,1:T(8,128)S(1)} fusion(f32[3,128,64,64]{1,2,3,0:T(8,128)} %get-tuple-element.10), kind=kOutput, calls=%fused_computation.16 | convolution fusion | flops 1208016896 | bytes 12582912 | tf_op jit(solution)/shard_map/...kb,bm->...mk/dot_general | solution.py:18
  827.8 10.2 %multiply_bitcast_fusion = f32[3,1,128,64,64]{2,3,4,0,1:T(8,128)S(1)} fusion(f32[64,3,128,64]{2,0,3,1:T(8,128)S(1)} %fusion.8, f32[3,128,64,64]{1,2,3,0:T(8,128)S(1)} %bitcast.357), kind=kOutput, calls=%fused_computation.20 | convolution fusion | flops 1211162624 | bytes 18874368 | tf_op jit(solution)/shard_map/...kb,bm->...mk/dot_general | solution.py:18
  838.0 6.3 copy.91
  844.3 6.6 copy.92
  (69 shorter events, 80.5 us)
Async XLA Ops:
  48.8 19.2 %slice-start = ((s8[6291456]{0:T(1024)(128)(4,1)}), s8[4194304]{0:T(1024)(128)(4,1)S(1)}, s32[]{:S(2)}) async-start(s8[6291456]{0:T(1024)(128)(4,1)} %bitcast.348), calls=%async_computation.4 | async-start | bytes 8388608
  58.3 9.7 %slice-start.1 = ((s8[6291456]{0:T(1024)(128)(4,1)}), s8[2097152]{0:T(1024)(128)(4,1)S(1)}, s32[]{:S(2)}) async-start(s8[6291456]{0:T(1024)(128)(4,1)} %bitcast.348), calls=%async_computation.5 | async-start | bytes 4194304
  272.5 53.6 %all-to-all-start.1 = ((f32[4,1,264192]{2,1,0:T(1,128)}), f32[4,1,264192]{2,1,0:T(1,128)}, u32[]{:S(2)}, u32[]{:S(2)}) async-start(f32[4,1,264192]{2,1,0:T(1,128)} %bitcast.366), calls=%async_computation.1 | async-start | bytes 8454144 | tf_op jit(solution)/shard_map/all_to_all | solution.py:135
  351.5 8.2 copy-start.3
  359.7 6.0 copy-start.4
  367.4 11.6 %slice-start.4 = ((s8[4227072]{0:T(1024)(128)(4,1)}), s8[32768]{0:T(1024)(128)(4,1)S(1)}, s32[]{:S(2)}) async-start(s8[4227072]{0:T(1024)(128)(4,1)} %bitcast.361), calls=%async_computation.8 | async-start | bytes 65536
  371.0 8.0 copy-start.2
  371.0 8.0 slice-start.5
  445.1 28.9 %copy-start = (f32[64,3,43,64]{3,0,2,1:T(8,128)}, f32[64,3,43,64]{3,0,2,1:T(8,128)S(1)}, u32[]{:S(2)}) copy-start(f32[64,3,43,64]{3,0,2,1:T(8,128)S(1)} %fusion.66) | copy-start | bytes 6340612
  449.6 24.4 %copy-start.1 = (f32[64,3,43,64]{3,0,2,1:T(8,128)}, f32[64,3,43,64]{3,0,2,1:T(8,128)S(1)}, u32[]{:S(2)}) copy-start(f32[64,3,43,64]{3,0,2,1:T(8,128)S(1)} %fusion.67) | copy-start | bytes 6340612
  615.5 99.0 %all-to-all-start.3 = ((f32[8,1,132096]{2,1,0:T(1,128)}), f32[8,1,132096]{2,1,0:T(1,128)}, u32[]{:S(2)}, u32[]{:S(2)}) async-start(f32[8,1,132096]{2,1,0:T(1,128)} %reshape.977), calls=%async_computation.3 | async-start | bytes 8454144 | tf_op jit(solution)/shard_map/all_to_all | solution.py:153
  815.1 12.6 %slice-start.2 = ((s8[6291456]{0:T(1024)(128)(4,1)}), s8[4194304]{0:T(1024)(128)(4,1)S(1)}, s32[]{:S(2)}) async-start(s8[6291456]{0:T(1024)(128)(4,1)} %bitcast.356), calls=%async_computation.6 | async-start | bytes 8388608
  815.1 12.6 %slice-start.3 = ((s8[6291456]{0:T(1024)(128)(4,1)}), s8[2097152]{0:T(1024)(128)(4,1)S(1)}, s32[]{:S(2)}) async-start(s8[6291456]{0:T(1024)(128)(4,1)} %bitcast.356), calls=%async_computation.7 | async-start | bytes 4194304
where the time goes:
time: 859 us; the launch traced here: 851 us
  matrix products  308 us (36%)
  local copies, waits for them, and re-layouts  198 us (23%)
  blocking collectives  154 us (18%)
  waiting for transfers between devices  141 us (16%)
  other arithmetic  39 us (5%)
  starting transfers between devices  9.87 us (1%)
    all_to_all x1, blocking collectives, local(): lax.all_to_all(first_send(spectrum, narrow_size), 'narrow', split_axis=0,...  102 us
    dot_general x8, matrix products, complex_product(): jnp.einsum(pattern, left_real, table_real, precision=highest)  96.5 us
    all_to_all x1, waiting for transfers between devices, local(): lax.all_to_all(outgoing, 'narrow', split_axis=0, concat_axis=1, tiled=True)  94.2 us
    dot_general x7, matrix products, complex_product(): jnp.einsum(pattern, left_real, table_imag, precision=highest)  76.1 us
    dot_general x8, matrix products, complex_product(): jnp.einsum(pattern, left_imag, table_imag, precision=highest)  74.8 us
    dot_general x7, matrix products, complex_product(): jnp.einsum(pattern, left_imag, table_real, precision=highest)  60.6 us
    all_to_all x1, blocking collectives, local(): lax.all_to_all(first_return(solved, narrow_size, wide_size, row_count), '...  52 us
    all_to_all x1, waiting for transfers between devices, local(): lax.all_to_all(outgoing, 'wide', split_axis=0, concat_axis=1, tiled=True)  47 us
  transfers between devices with their start and end apart: 2, of which 2 were waited for; matrix products, arithmetic and copies ran while one was open for 0% of the time, Pallas kernels for 0%

commit v1 on v0

--- a/solution.py
+++ b/solution.py
@@ -6,6 +6,12 @@
 
 radix_split = 64
 highest = lax.Precision.HIGHEST
+
+
+def stacked_exchange(block, mesh_axis, split, join):
+    pieces = jnp.split(block, lax.axis_size(mesh_axis), axis=split)
+    received = lax.all_to_all(jnp.stack(pieces), mesh_axis, 0, 0)
+    return jnp.concatenate(received, axis=join)
 
 
 def angle_tables(row_size, col_size, period, direction):
@@ -132,7 +138,7 @@
         first_send(spectrum, narrow_size), "narrow", split_axis=0, concat_axis=1, tiled=True
     )
     outgoing = second_send(halfway, narrow_size, wide_size, groups, row_count, per_device)
-    arrived = lax.all_to_all(outgoing, "wide", split_axis=0, concat_axis=1, tiled=True)
+    arrived = stacked_exchange(outgoing, "wide", 0, 1)
     lines = arrange_lines(arrived, narrow_size, wide_size, groups, row_count, per_device)
     line_start = (
         lax.axis_index("narrow") * (per_device * wide_size) + lax.axis_index("wide") * per_device

time: 859 us -> 900 us (1.048)
  local copies, waits for them, and re-layouts: 198 us -> 231 us
    split x0 -> x5, local copies, waits for them, and re-layouts: none -> 42.1 us  [stacked_exchange(): pieces = jnp.split(block, lax.axis_size(mesh_axis), axis=split)]
    transpose x1 -> x0, local copies, waits for them, and re-layouts: 9.21 us -> none  [second_send(): return shaped.transpose(3, 1, 4, 0, 2).reshape(second_size, 1, -1)]
where the time goes in v1:
time: 900 us; the launch traced here: 892 us
  matrix products  308 us (34%)
  local copies, waits for them, and re-layouts  231 us (26%)
  blocking collectives  154 us (17%)
  waiting for transfers between devices  141 us (16%)
  other arithmetic  47.1 us (5%)
  starting transfers between devices  9.66 us (1%)
    all_to_all x1, blocking collectives, local(): lax.all_to_all(first_send(spectrum, narrow_size), 'narrow', split_axis=0,...  102 us
    dot_general x8, matrix products, complex_product(): jnp.einsum(pattern, left_real, table_real, precision=highest)  96.5 us
    all_to_all x1, waiting for transfers between devices, local(): lax.all_to_all(outgoing, 'narrow', split_axis=0, concat_axis=1, tiled=True)  94.2 us
    dot_general x7, matrix products, complex_product(): jnp.einsum(pattern, left_real, table_imag, precision=highest)  76.1 us
    dot_general x8, matrix products, complex_product(): jnp.einsum(pattern, left_imag, table_imag, precision=highest)  74.8 us
    dot_general x7, matrix products, complex_product(): jnp.einsum(pattern, left_imag, table_real, precision=highest)  60.6 us
    all_to_all x1, blocking collectives, local(): lax.all_to_all(first_return(solved, narrow_size, wide_size, row_count), '...  52 us
    all_to_all x1, waiting for transfers between devices, stacked_exchange(): received = lax.all_to_all(jnp.stack(pieces), mesh_axis, 0, 0)  47 us
  transfers between devices with their start and end apart: 2, of which 2 were waited for; matrix products, arithmetic and copies ran while one was open for 0% of the time, Pallas kernels for 0%

profile of v1, /device:TPU:0, one launch (start us, length us, event | category | flops | bytes accessed | tf_op | source)
XLA Modules:
  0.0 892.1 jit_solution(9983868670534154288)
XLA Ops:
  9.5 6.6 copy.58
  16.1 13.6 %fusion.28 = f32[64,3,128,64]{2,0,3,1:T(8,128)} fusion(f32[3,128,64,64]{1,3,2,0:T(8,128)} %bitcast.349), kind=kOutput, calls=%fused_computation.39 | convolution fusion | flops 1208016896 | bytes 12582912 | tf_op jit(solution)/shard_map/...ab,ak->...kb/dot_general | solution.py:27
  29.7 19.1 %fusion.5 = (f32[3,128,64,64]{1,2,3,0:T(8,128)}, f32[3,128,64,64]{1,2,3,0:T(8,128)S(1)}) fusion(f32[64,64]{0,1:T(8,128)S(1)} %get-tuple-element.29, f32[64,64]{0,1:T(8,128)S(1)} %get-tuple-element.30, f32[64,3,128,64]{2,0,3,1:T(8,128)} %fusion.28, f32[64,3,128,64]{2,0,3,1:T(8,128)} %fusion.52, f32[64,3,128,64]{2,0,3,1:T(8,128)} %fusion.54, ...), kind=kOutput, calls=%fused_computation.11 | convolution fusion | flops 1220599808 | bytes 37781504 | tf_op jit(solution)/shard_map/...ab,ak->...kb/dot_general | solution.py:24
  48.8 9.5 %fusion.22 = f32[64,3,128,64]{2,0,3,1:T(8,128)S(1)} fusion(f32[3,128,64,64]{1,2,3,0:T(8,128)S(1)} %get-tuple-element.12), kind=kOutput, calls=%fused_computation.33 | convolution fusion | flops 1208016896 | bytes 12582912 | tf_op jit(solution)/shard_map/...kb,bm->...mk/dot_general | solution.py:24
  58.3 9.6 %fusion.20 = f32[64,3,128,64]{2,0,3,1:T(8,128)S(1)} fusion(f32[3,128,64,64]{1,2,3,0:T(8,128)S(1)} %get-tuple-element.12), kind=kOutput, calls=%fused_computation.31 | convolution fusion | flops 1208016896 | bytes 12582912 | tf_op jit(solution)/shard_map/...kb,bm->...mk/dot_general | solution.py:27
  68.0 9.7 %subtract_bitcast_fusion = f32[3,1,128,64,64]{2,3,4,0,1:T(8,128)S(1)} fusion(f32[64,3,128,64]{2,0,3,1:T(8,128)S(1)} %fusion.22, f32[3,128,64,64]{1,2,3,0:T(8,128)S(1)} %bitcast.352), kind=kOutput, calls=%fused_computation.22 | convolution fusion | flops 1209589760 | bytes 18874368 | tf_op jit(solution)/shard_map/...kb,bm->...mk/dot_general | solution.py:24
  81.5 10.0 %add_bitcast_fusion = f32[3,1,128,64,64]{2,3,4,0,1:T(8,128)S(1)} fusion(f32[64,3,128,64]{2,0,3,1:T(8,128)S(1)} %fusion.20, f32[3,128,64,64]{1,2,3,0:T(8,128)S(1)} %bitcast.352), kind=kOutput, calls=%fused_computation.21 | convolution fusion | flops 1209589760 | bytes 18874368 | tf_op jit(solution)/shard_map/...kb,bm->...mk/dot_general | solution.py:27
  102.9 6.1 copy.68
  109.1 11.9 %reshape.973 = f32[8,1,132096]{2,1,0:T(1,128)} reshape(f32[8,6,128,172]{3,2,1,0:T(8,128)} %copy.68) | data formatting | bytes 8454144 | tf_op jit(solution)/shard_map/reshape | solution.py:89
  121.0 102.0 %all_to_all.32 = f32[8,1,132096]{2,1,0:T(1,128)} all-to-all(f32[8,1,132096]{2,1,0:T(1,128)} %reshape.973), channel_id=1, replica_groups=mesh['wide'=4,'narrow'=8] {'narrow'}, dimensions={0} | all-to-all | bytes 8454144 | tf_op jit(solution)/shard_map/all_to_all | solution.py:137
  223.0 13.4 %reduce = f32[8,132096]{1,0:T(8,128)} reduce(f32[8,1,132096]{2,1,0:T(1,128)} %all_to_all.32, f32[]{:T(128)} %constant.129), dimensions={1}, to_apply=%all_to_all.8.reduce_sub_computation | reduce | bytes 8454148 | tf_op jit(solution)/shard_map/all_to_all | solution.py:137
  236.4 26.8 %reshape.952 = f32[8,6,128,4,43]{4,3,2,1,0:T(4,128)} reshape(f32[8,132096]{1,0:T(8,128)} %reduce) | data formatting | bytes 8454144 | tf_op jit(solution)/shard_map/reshape | solution.py:94
  263.3 23.5 %fusion.259 = (f32[1,6,43,8,128]{2,0,4,1,3:T(1,128)}, f32[1,6,43,8,128]{2,0,4,1,3:T(1,128)S(1)}, f32[1,6,43,8,128]{2,0,4,1,3:T(1,128)}, f32[1,6,43,8,128]{2,0,4,1,3:T(1,128)}) fusion(f32[4,6,43,8,128]{2,0,4,1,3:T(4,128)} %bitcast.357), kind=kLoop, calls=%fused_computation.299 | loop fusion | bytes 8454144 | tf_op jit(solution)/shard_map/split | solution.py:12
  286.8 5.2 copy.70
  297.2 5.2 copy.72
  305.4 8.1 pad_maximum_fusion
  319.9 47.0 %all-to-all-done.1 = f32[4,1,1,264192]{3,2,1,0:T(1,128)} async-done(((f32[4,1,1,264192]{3,2,1,0:T(1,128)}), f32[4,1,1,264192]{3,2,1,0:T(1,128)}, u32[]{:S(2)}, u32[]{:S(2)}) %all-to-all-start.1) | async-done | bytes 4227104 | tf_op jit(solution)/shard_map/all_to_all | solution.py:13
  371.7 5.9 reshape_reshape.17
  377.6 9.3 %fusion.260 = (f32[3,1,1,43,4096]{4,1,0,3,2:T(1,128)}, f32[3,1,1,43,4096]{4,1,0,3,2:T(1,128)S(1)}) fusion(f32[3,2,1,43,4096]{4,1,0,3,2:T(2,128)} %reshape_reshape.17), kind=kLoop, calls=%fused_computation.300 | loop fusion | bytes 8454144 | tf_op jit(solution)/shard_map/slice | solution.py:56
  392.3 8.2 fusion.107
  400.5 6.0 fusion.97
  411.9 7.9 convolution_subtract_fusion
  424.3 11.3 %fusion.42 = f32[64,3,43,64]{3,0,2,1:T(8,128)S(1)} fusion(f32[64,3,43,64]{3,0,2,1:T(8,128)S(1)} %convolution_add_fusion, f32[64,3,43,64]{3,0,2,1:T(8,128)S(1)} %convolution_subtract_fusion, f32[64,64]{1,0:T(8,128)S(1)} %copy.78, f32[64,64]{1,0:T(8,128)S(1)} %copy.77), kind=kOutput, calls=%fused_computation.61 | convolution fusion | flops 407441408 | bytes 6373376 | tf_op jit(solution)/shard_map/...kb,bm->...mk/dot_general | solution.py:27
  435.6 11.5 %fusion.44 = f32[64,3,43,64]{3,0,2,1:T(8,128)S(1)} fusion(f32[64,3,43,64]{3,0,2,1:T(8,128)S(1)} %convolution_add_fusion, f32[64,3,43,64]{3,0,2,1:T(8,128)S(1)} %convolution_subtract_fusion, f32[64,64]{1,0:T(8,128)S(1)} %copy.78, f32[64,64]{1,0:T(8,128)S(1)} %copy.77), kind=kOutput, calls=%fused_computation.63 | convolution fusion | flops 407441408 | bytes 6373376 | tf_op jit(solution)/shard_map/...kb,bm->...mk/dot_general | solution.py:24
  447.1 11.1 %add_bitcast_fusion.1 = f32[3,1,43,64,64]{4,3,2,0,1:T(8,128)S(1)} fusion(f32[64,3,43,64]{3,0,2,1:T(8,128)S(1)} %fusion.42, f32[64,3,43,64]{3,0,2,1:T(8,128)S(1)} %convolution_add_fusion, f32[64,3,43,64]{3,0,2,1:T(8,128)S(1)} %convolution_subtract_fusion, f32[64,64]{1,0:T(8,128)S(1)} %copy.78, f32[64,64]{1,0:T(8,128)S(1)} %copy.77), kind=kOutput, calls=%fused_computation.78 | convolution fusion | flops 407969792 | bytes 8486912 | tf_op jit(solution)/shard_map/...kb,bm->...mk/dot_general | solution.py:27
  458.3 11.3 %subtract_bitcast_fusion.1 = f32[3,1,43,64,64]{4,3,2,0,1:T(8,128)S(1)} fusion(f32[64,3,43,64]{3,0,2,1:T(8,128)S(1)} %fusion.44, f32[64,3,43,64]{3,0,2,1:T(8,128)S(1)} %convolution_add_fusion, f32[64,3,43,64]{3,0,2,1:T(8,128)S(1)} %convolution_subtract_fusion, f32[64,64]{1,0:T(8,128)S(1)} %copy.78, f32[64,64]{1,0:T(8,128)S(1)} %copy.77), kind=kOutput, calls=%fused_computation.79 | convolution fusion | flops 407969792 | bytes 8486912 | tf_op jit(solution)/shard_map/...kb,bm->...mk/dot_general | solution.py:24
  490.4 11.3 %fusion.34 = f32[64,3,43,64]{3,0,2,1:T(8,128)S(1)} fusion(f32[64,3,43,64]{3,0,2,1:T(8,128)S(1)} %fusion.67, f32[64,3,43,64]{3,0,2,1:T(8,128)S(1)} %fusion.66, f32[64,64]{1,0:T(8,128)S(1)} %copy.82, f32[64,64]{1,0:T(8,128)S(1)} %copy.81), kind=kOutput, calls=%fused_computation.49 | convolution fusion | flops 407441408 | bytes 6373376 | tf_op jit(solution)/shard_map/...kb,bm->...mk/dot_general | solution.py:24
  501.7 13.1 %fusion.32 = f32[64,3,43,64]{3,0,2,1:T(8,128)} fusion(f32[64,3,43,64]{3,0,2,1:T(8,128)S(1)} %fusion.67, f32[64,3,43,64]{3,0,2,1:T(8,128)S(1)} %fusion.66, f32[64,64]{1,0:T(8,128)S(1)} %copy.82, f32[64,64]{1,0:T(8,128)S(1)} %copy.81), kind=kOutput, calls=%fused_computation.47 | convolution fusion | flops 407441408 | bytes 6373376 | tf_op jit(solution)/shard_map/...kb,bm->...mk/dot_general | solution.py:27
  514.8 13.3 %multiply_bitcast_fusion.2 = f32[3,1,43,64,64]{4,3,2,0,1:T(8,128)} fusion(f32[64,3,43,64]{3,0,2,1:T(8,128)S(1)} %fusion.34, f32[64,3,43,64]{3,0,2,1:T(8,128)S(1)} %fusion.67, f32[64,3,43,64]{3,0,2,1:T(8,128)S(1)} %fusion.66, f32[64,64]{1,0:T(8,128)S(1)} %copy.82, f32[64,64]{1,0:T(8,128)S(1)} %copy.81), kind=kOutput, calls=%fused_computation.77 | convolution fusion | flops 408498176 | bytes 8486912 | tf_op jit(solution)/shard_map/...kb,bm->...mk/dot_general | solution.py:24
  533.1 17.7 %multiply_bitcast_fusion.1 = f32[3,1,43,64,64]{4,3,2,0,1:T(8,128)} fusion(f32[64,3,43,64]{3,0,2,1:T(8,128)} %fusion.32, f32[64,3,43,64]{3,0,2,1:T(8,128)} %copy-done.1, f32[64,3,43,64]{3,0,2,1:T(8,128)} %copy-done, f32[64,64]{1,0:T(8,128)S(1)} %copy.82, f32[64,64]{1,0:T(8,128)S(1)} %copy.81), kind=kOutput, calls=%fused_computation.76 | convolution fusion | flops 408498176 | bytes 8486912 | tf_op jit(solution)/shard_map/...kb,bm->...mk/dot_general | solution.py:27
  550.9 5.7 div.205
  556.5 5.9 pad_maximum_fusion.1
  566.1 6.7 reshape_reshape.18
  575.2 52.0 %all_to_all.33 = f32[4,1,264192]{2,1,0:T(1,128)} all-to-all(f32[4,1,264192]{2,1,0:T(1,128)S(1)} %bitcast.368), channel_id=1, replica_groups=mesh['wide'=4,'narrow'=8] {'wide'}, dimensions={0} | all-to-all | bytes 8454144 | tf_op jit(solution)/shard_map/all_to_all | solution.py:151
  627.2 9.0 %copy.86 = f32[4,6,43,8,128]{2,0,4,1,3:T(4,128)} copy(f32[4,6,43,8,128]{4,3,2,1,0:T(8,128)} %bitcast.369) | data formatting | bytes 8454144 | tf_op jit(solution)/shard_map/reshape | solution.py:113
  636.2 20.3 %reshape.974 = f32[8,1,132096]{2,1,0:T(1,128)} reshape(f32[8,6,128,4,43]{4,3,2,1,0:T(4,128)} %bitcast.358) | data formatting | bytes 8454144 | tf_op jit(solution)/shard_map/reshape | solution.py:114
  661.2 94.2 %all-to-all-done.3 = f32[8,1,132096]{2,1,0:T(1,128)} async-done(((f32[8,1,132096]{2,1,0:T(1,128)}), f32[8,1,132096]{2,1,0:T(1,128)}, u32[]{:S(2)}, u32[]{:S(2)}) %all-to-all-start.3) | async-done | bytes 4227104 | tf_op jit(solution)/shard_map/all_to_all | solution.py:159
  755.5 13.2 %reduce.1 = f32[8,132096]{1,0:T(8,128)} reduce(f32[8,1,132096]{2,1,0:T(1,128)} %all-to-all-done.3, f32[]{:T(128)} %constant.129), dimensions={1}, to_apply=%all_to_all.11.reduce_sub_computation | reduce | bytes 8454148 | tf_op jit(solution)/shard_map/all_to_all | solution.py:159
  768.7 13.7 %reshape.964 = f32[8,6,128,172]{3,2,1,0:T(8,128)} reshape(f32[8,132096]{1,0:T(8,128)} %reduce.1) | data formatting | bytes 8454144 | tf_op jit(solution)/shard_map/reshape | solution.py:118
  782.4 6.0 copy.88
  796.2 13.5 %fusion.12 = f32[64,3,128,64]{2,0,3,1:T(8,128)} fusion(f32[3,128,64,64]{1,3,2,0:T(8,128)S(1)} %bitcast.355), kind=kOutput, calls=%fused_computation.23 | convolution fusion | flops 1208016896 | bytes 12582912 | tf_op jit(solution)/shard_map/...ab,ak->...kb/dot_general | solution.py:27
  809.6 13.0 %fusion.14 = f32[64,3,128,64]{2,0,3,1:T(8,128)} fusion(f32[3,128,64,64]{1,3,2,0:T(8,128)S(1)} %bitcast.356), kind=kOutput, calls=%fused_computation.25 | convolution fusion | flops 1208016896 | bytes 12582912 | tf_op jit(solution)/shard_map/...ab,ak->...kb/dot_general | solution.py:24
  823.0 13.2 %fusion.16 = f32[64,3,128,64]{2,0,3,1:T(8,128)} fusion(f32[3,128,64,64]{1,3,2,0:T(8,128)S(1)} %bitcast.353), kind=kOutput, calls=%fused_computation.27 | convolution fusion | flops 1208016896 | bytes 12582912 | tf_op jit(solution)/shard_map/...ab,ak->...kb/dot_general | solution.py:27
  836.2 19.8 %fusion.1 = (f32[3,128,64,64]{1,2,3,0:T(8,128)}, f32[3,128,64,64]{1,2,3,0:T(8,128)}) fusion(f32[64,64]{0,1:T(8,128)S(1)} %get-tuple-element.31, f32[64,64]{0,1:T(8,128)S(1)} %get-tuple-element.32, f32[64,3,128,64]{2,0,3,1:T(8,128)} %fusion.16, f32[64,3,128,64]{2,0,3,1:T(8,128)} %fusion.12, f32[64,3,128,64]{2,0,3,1:T(8,128)} %fusion.14, ...), kind=kOutput, calls=%fused_computation.3 | convolution fusion | flops 1220599808 | bytes 37781504 | tf_op jit(solution)/shard_map/...ab,ak->...kb/dot_general | solution.py:24
  856.0 12.6 %fusion.8 = f32[64,3,128,64]{2,0,3,1:T(8,128)S(1)} fusion(f32[3,128,64,64]{1,2,3,0:T(8,128)} %get-tuple-element.10), kind=kOutput, calls=%fused_computation.16 | convolution fusion | flops 1208016896 | bytes 12582912 | tf_op jit(solution)/shard_map/...kb,bm->...mk/dot_general | solution.py:24
  868.7 10.2 %multiply_bitcast_fusion = f32[3,1,128,64,64]{2,3,4,0,1:T(8,128)S(1)} fusion(f32[64,3,128,64]{2,0,3,1:T(8,128)S(1)} %fusion.8, f32[3,128,64,64]{1,2,3,0:T(8,128)S(1)} %bitcast.360), kind=kOutput, calls=%fused_computation.20 | convolution fusion | flops 1211162624 | bytes 18874368 | tf_op jit(solution)/shard_map/...kb,bm->...mk/dot_general | solution.py:24
  878.9 6.3 copy.96
  885.2 6.6 copy.97
  (74 shorter events, 103.4 us)
Async XLA Ops:
  48.8 19.2 %slice-start = ((s8[6291456]{0:T(1024)(128)(4,1)}), s8[4194304]{0:T(1024)(128)(4,1)S(1)}, s32[]{:S(2)}) async-start(s8[6291456]{0:T(1024)(128)(4,1)} %bitcast.351), calls=%async_computation.4 | async-start | bytes 8388608
  58.3 9.7 %slice-start.1 = ((s8[6291456]{0:T(1024)(128)(4,1)}), s8[2097152]{0:T(1024)(128)(4,1)S(1)}, s32[]{:S(2)}) async-start(s8[6291456]{0:T(1024)(128)(4,1)} %bitcast.351), calls=%async_computation.5 | async-start | bytes 4194304
  313.5 53.4 %all-to-all-start.1 = ((f32[4,1,1,264192]{3,2,1,0:T(1,128)}), f32[4,1,1,264192]{3,2,1,0:T(1,128)}, u32[]{:S(2)}, u32[]{:S(2)}) async-start(f32[4,1,1,264192]{3,2,1,0:T(1,128)} %pad_maximum_fusion), calls=%async_computation.1 | async-start | bytes 8454144 | tf_op jit(solution)/shard_map/all_to_all | solution.py:13
  392.3 8.2 copy-start.3
  400.5 6.0 copy-start.4
  408.2 11.6 %slice-start.4 = ((s8[4227072]{0:T(1024)(128)(4,1)}), s8[32768]{0:T(1024)(128)(4,1)S(1)}, s32[]{:S(2)}) async-start(s8[4227072]{0:T(1024)(128)(4,1)} %bitcast.364), calls=%async_computation.8 | async-start | bytes 65536
  411.9 8.0 copy-start.2
  411.9 8.0 slice-start.5
  485.9 28.9 %copy-start = (f32[64,3,43,64]{3,0,2,1:T(8,128)}, f32[64,3,43,64]{3,0,2,1:T(8,128)S(1)}, u32[]{:S(2)}) copy-start(f32[64,3,43,64]{3,0,2,1:T(8,128)S(1)} %fusion.66) | copy-start | bytes 6340612
  490.4 24.4 %copy-start.1 = (f32[64,3,43,64]{3,0,2,1:T(8,128)}, f32[64,3,43,64]{3,0,2,1:T(8,128)S(1)}, u32[]{:S(2)}) copy-start(f32[64,3,43,64]{3,0,2,1:T(8,128)S(1)} %fusion.67) | copy-start | bytes 6340612
  656.4 99.0 %all-to-all-start.3 = ((f32[8,1,132096]{2,1,0:T(1,128)}), f32[8,1,132096]{2,1,0:T(1,128)}, u32[]{:S(2)}, u32[]{:S(2)}) async-start(f32[8,1,132096]{2,1,0:T(1,128)} %reshape.974), calls=%async_computation.3 | async-start | bytes 8454144 | tf_op jit(solution)/shard_map/all_to_all | solution.py:159
  856.0 12.6 %slice-start.2 = ((s8[6291456]{0:T(1024)(128)(4,1)}), s8[4194304]{0:T(1024)(128)(4,1)S(1)}, s32[]{:S(2)}) async-start(s8[6291456]{0:T(1024)(128)(4,1)} %bitcast.359), calls=%async_computation.6 | async-start | bytes 8388608
  856.0 12.6 %slice-start.3 = ((s8[6291456]{0:T(1024)(128)(4,1)}), s8[2097152]{0:T(1024)(128)(4,1)S(1)}, s32[]{:S(2)}) async-start(s8[6291456]{0:T(1024)(128)(4,1)} %bitcast.359), calls=%async_computation.7 | async-start | bytes 4194304
